TPU v7x, 256 devices: a 8x8x2 block of a 8x8x16 slice. The times are simulated.
256 devices in a mesh: groups: 2 (over z), expert: 64 (over y, x), tensor: 2 (over core).
Axes of the slice: x: 8, y: 8, z: 2, core: 2. Of those that a mesh axis runs over, the one named last changes fastest.
The devices are a block of a 8x8x16 slice.
Arguments:
- hidden_in: bfloat16 [2048, 3584], P(('groups', 'expert')), parts along dimension 0, may hold values from -6 to 6
- batch_len: int32 [2], P('groups'), parts along dimension 0, may hold values from 256 to 1024
- expert_ids: int32 [2048, 8], P(('groups', 'expert')), parts along dimension 0, may hold values from 0 to 63, all different within a row; in each aligned block of 16 rows (0 to 15, 16 to 31, ...) at most 3 rows name the same one
- gate_num: int32 [2048, 8], P(('groups', 'expert')), parts along dimension 0, may hold values from 1 to 1024
- w_gate: bfloat16 [64, 3584, 1024], P('expert', None, 'tensor'), may hold values from -0.09375 to 0.09375
- w_up: bfloat16 [64, 3584, 1024], P('expert', None, 'tensor'), may hold values from -0.09375 to 0.09375
- w_down: bfloat16 [64, 1024, 3584], P('expert', 'tensor'), may hold values from -0.1875 to 0.1875
- q_latent: bfloat16 [4, 64, 512], P('groups', 'tensor'), parts along dimension 0, may hold values from -117 to 117
- q_rope: bfloat16 [4, 64, 64], P('groups', 'tensor'), parts along dimension 0, may hold values from -6 to 6
- kv_latent: bfloat16 [4, 8192, 512], P('groups', 'expert'), parts along dimension 0, may hold values from -4 to 4
- kv_rope: bfloat16 [4, 64, 8192], P('groups', None, 'expert'), parts along dimension 0, may hold values from -4 to 4
- ctx_len: int32 [4], P('groups'), parts along dimension 0, may hold values from 1 to 8192, as said below
Outputs:
- moe_out: bfloat16 [2048, 3584], P(('groups', 'expert')), parts along dimension 0
- attn_out: bfloat16 [4, 64, 512], P('groups', 'tensor'), parts along dimension 0
There are 2 independent parts, one for each index of `groups`. A program takes and returns all parts, laid end to end along the dimension named above; an argument that names none is the same for every part. Nothing has to cross between parts.
Inputs may be any that keep to these rules, and one draw needn't show every extreme that they name: `expert_ids`: each row names 8 different experts; the 16 rows of one index of the expert axis name any one expert at most 3 times. `batch_len`: the live slots are the first ones of the replica. `ctx_len`: the first request's context fills all 8192 positions.
All inputs are finite; a program needn't handle non-finite values.
Results may differ from a plain program's by a relative error of at most 0.0028.
The roundings to bfloat16 on the way count: a program that leaves them out, or rounds other values in their place, can miss the bound.
Values may be sent and summed in bfloat16 or wider, within the bound.
A program may use at most 64 MiB of HBM per device.

v0:
```python
import jax
import jax.numpy as jnp
from jax import lax
from jax.sharding import Mesh
from jax.sharding import PartitionSpec as P

EXPERT = ("expert_0", "expert_1")
GROUPS_EXPERT = ("groups", "expert_0", "expert_1")


gate_denominator = 1024.0
softmax_scale = 192.0 ** (-0.5)


def joined_along(parts, dim):
    parts = jnp.moveaxis(parts, 0, dim)
    shape = parts.shape
    return parts.reshape(*shape[:dim], shape[dim] * shape[dim + 1], *shape[dim + 2 :])


def sent_to_all(value, axis):
    copies = jnp.broadcast_to(value, (lax.axis_size(axis), *value.shape))
    return lax.all_to_all(copies, axis, split_axis=0, concat_axis=0, tiled=True)


def gathered_copies(value, axis, dim):
    return joined_along(sent_to_all(value, axis), dim)


def exchange_in_groups(value, axis, split_dim, concat_dim, work, item_dim, out_dim):
    items = jax.tree.leaves(value)[0].shape[item_dim]
    count = 2 if items % 2 == 0 else 1
    finished = []
    for k in range(count):
        group = jax.tree.map(
            lambda a: lax.slice_in_dim(
                a, k * (items // count), (k + 1) * (items // count), axis=item_dim
            ),
            value,
        )
        finished.append(
            work(
                lax.all_to_all(
                    group, axis, split_axis=split_dim, concat_axis=concat_dim, tiled=True
                )
            )
        )
    return jax.tree.map(lambda *parts: jnp.concatenate(parts, axis=out_dim), *finished)


def in_blocks(value, dim, size):
    shape = value.shape
    parts = value.reshape(*shape[:dim], size, shape[dim] // size, *shape[dim + 1 :])
    return jnp.moveaxis(parts, dim, 0)


def summed_on_arrival(value, axis, dim):
    parts = in_blocks(value, dim, lax.axis_size(axis))
    arrived = lax.all_to_all(parts, axis, split_axis=0, concat_axis=0, tiled=True)
    return arrived.sum(axis=0)


def collected_together(value, axis):
    leaves = jax.tree.leaves(value)
    order = sorted(range(len(leaves)), key=lambda k: -leaves[k].size)
    width = (1, *leaves[order[0]].shape)[-1]
    lines = [
        jnp.pad(leaves[k].reshape(-1), (0, -leaves[k].size % width)).reshape(-1, width)
        for k in order
    ]
    both, at, found = (lax.all_gather(jnp.concatenate(lines), axis), 0, {})
    for k, line in zip(order, lines):
        slab = both[:, at : at + len(line)].reshape(len(both), -1)
        found[k] = slab[:, : leaves[k].size].reshape(-1, *leaves[k].shape)
        at += len(line)
    numbers = iter(range(len(leaves)))
    return jax.tree.map(lambda _: found[next(numbers)], value)


def combined_by_axis(value, axes, combine):
    for axis in axes:
        pieces = collected_together(value, axis)
        value = jax.tree.map(lambda part: part[0], pieces)
        for k in range(1, lax.axis_size(axis)):
            value = combine(value, jax.tree.map(lambda part: part[k], pieces))
    return value


def join_parts(first, second):
    peak = jnp.maximum(first[0], second[0])
    left = jnp.exp(first[0] - peak)
    right = jnp.exp(second[0] - peak)
    total = first[1] * left + second[1] * right
    weighted = first[2] * left[..., None] + second[2] * right[..., None]
    return (peak, total, weighted)


def local(
    hidden_in,
    batch_len,
    expert_ids,
    gate_num,
    w_gate,
    w_up,
    w_down,
    q_latent,
    q_rope,
    kv_latent,
    kv_rope,
    ctx_len,
):
    owners = lax.axis_size(EXPERT)
    tok_rows, width = hidden_in.shape
    topk = expert_ids.shape[1]
    capacity = min(tok_rows, max(2, 3 * tok_rows * topk // (2 * owners)))
    first_row = lax.axis_index(EXPERT) * tok_rows
    live = first_row + jnp.arange(tok_rows, dtype=jnp.int32) < batch_len[0]
    flat_expert = expert_ids.reshape(-1)
    live_pick = jnp.repeat(live, topk)
    onehot = (
        (flat_expert[:, None] == jnp.arange(owners, dtype=jnp.int32)[None, :]) & live_pick[:, None]
    ).astype(jnp.int32)
    ranking = jnp.cumsum(onehot, axis=0) - 1
    slot = jnp.sum(onehot * ranking, axis=1)
    target = jnp.where(live_pick, flat_expert * capacity + slot, owners * capacity)
    half_width = width // lax.axis_size("tensor")
    source = lax.dynamic_slice_in_dim(
        hidden_in, lax.axis_index("tensor") * half_width, half_width, 1
    )
    picked = jnp.repeat(source, topk, axis=0)
    packed = (
        jnp.zeros((owners * capacity, source.shape[1]), jnp.bfloat16)
        .at[target]
        .set(picked, mode="drop")
    )
    packed = packed.reshape(owners, capacity, source.shape[1])

    def expert_rows(rows):
        rows = gathered_copies(rows, "tensor", 2)
        count = rows.shape[1]
        flat = rows.reshape(-1, width)
        gate = jnp.dot(flat, w_gate[0], preferred_element_type=jnp.float32)
        upper = jnp.dot(flat, w_up[0], preferred_element_type=jnp.float32)
        hidden = (jax.nn.silu(gate) * upper).astype(jnp.bfloat16)
        return jnp.dot(hidden, w_down[0], preferred_element_type=jnp.float32).reshape(
            owners, count, width
        )

    partial_value = exchange_in_groups(packed, EXPERT, 0, 0, expert_rows, 1, 1)
    weight = jnp.where(live_pick, gate_num.reshape(-1).astype(jnp.float32) / gate_denominator, 0.0)
    back_index = jnp.where(live_pick, target, 0)
    share = summed_on_arrival(partial_value, "tensor", 2).astype(jnp.bfloat16)
    back = lax.all_to_all(share, EXPERT, split_axis=0, concat_axis=0, tiled=True)
    rows = back.reshape(owners * capacity, back.shape[2])[back_index].astype(jnp.float32)
    scaled = (rows * weight[:, None]).reshape(tok_rows, topk, back.shape[2])
    moe_out = gathered_copies(jnp.sum(scaled, axis=1).astype(jnp.bfloat16), "tensor", 1)
    ctx_dev = kv_latent.shape[1]
    position = lax.axis_index(EXPERT) * ctx_dev + jnp.arange(ctx_dev, dtype=jnp.int32)
    valid_pos = position[None, :] < ctx_len[:, None]
    scores = jnp.einsum("bhl,bpl->bhp", q_latent, kv_latent, preferred_element_type=jnp.float32)
    scores = scores + jnp.einsum(
        "bhr,brp->bhp", q_rope, kv_rope, preferred_element_type=jnp.float32
    )
    scores = jnp.where(valid_pos[:, None, :], scores * softmax_scale, -1e30)
    peak = jnp.max(scores, axis=2)
    probs = jnp.where(valid_pos[:, None, :], jnp.exp(scores - peak[..., None]), 0.0)
    total = jnp.sum(probs, axis=2)
    weighted = jnp.einsum(
        "bhp,bpl->bhl", probs.astype(jnp.bfloat16), kv_latent, preferred_element_type=jnp.float32
    )
    peak, total, weighted = combined_by_axis((peak, total, weighted), EXPERT, join_parts)
    attn_out = (weighted / total[..., None]).astype(jnp.bfloat16)
    return (moe_out, attn_out)


def solution(mesh):
    finer = Mesh(
        mesh.devices.reshape(mesh.shape["groups"], 8, 8, mesh.shape["tensor"]),
        ("groups", "expert_0", "expert_1", "tensor"),
    )
    in_specs = (
        P(GROUPS_EXPERT, None),
        P("groups"),
        P(GROUPS_EXPERT, None),
        P(GROUPS_EXPERT, None),
        P(EXPERT, None, "tensor"),
        P(EXPERT, None, "tensor"),
        P(EXPERT, "tensor", None),
        P("groups", "tensor", None),
        P("groups", "tensor", None),
        P("groups", EXPERT, None),
        P("groups", None, EXPERT),
        P("groups"),
    )
    out_specs = (P(GROUPS_EXPERT, None), P("groups", "tensor", None))
    return jax.shard_map(local, mesh=finer, in_specs=in_specs, out_specs=out_specs, check_vma=False)
```

profile of v0, /device:TPU:513, one launch (start us, length us, event | category | flops | bytes accessed | tf_op | source)
XLA Modules:
  0.0 166.3 jit_solution(2754419291117256892)
XLA Ops:
  7.3 0.9 copy-done
  8.1 1.0 fusion.91
  9.1 0.8 broadcast_compare_fusion
  9.9 1.0 fusion.90
  11.0 0.2 fusion.41
  11.1 0.2 fusion.43
  11.4 0.7 maximum_bitcast_fusion
  12.2 0.7 broadcast_multiply_fusion
  12.9 0.8 copy.53
  14.4 0.1 reshape.986
  14.5 0.1 and.13
  14.7 0.1 mul.454
  14.8 0.1 fusion.40
  15.0 0.2 reduce_window_sum.11
  15.1 0.2 select_reduce_fusion
  15.3 0.8 constant_dynamic-slice_fusion
  16.2 1.5 scatter_custom_fusion
  17.7 1.2 reshape.988
  18.8 21.8 %all-to-all-start = ((bf16[64,3,1792]{2,1,0:T(4,128)(2,1)}), bf16[64,3,1792]{2,1,0:T(4,128)(2,1)S(1)}, u32[]{:S(2)}, u32[]{:S(2)}) async-start(bf16[64,3,1792]{2,1,0:T(4,128)(2,1)} %reshape.988), calls=%async_computation | async-start | bytes 1835008 | tf_op jit(solution)/shard_map/all_to_all | solution.py:43
  40.7 5.9 %copy.67 = bf16[3584,512]{1,0:T(8,128)(2,1)} copy(bf16[3584,512]{0,1:T(8,128)(2,1)} %bitcast.322) | data formatting | bytes 7340032 | tf_op jit(solution)/shard_map/dot_general | solution.py:145
  46.6 13.1 %all-to-all-done = bf16[64,3,1792]{2,1,0:T(4,128)(2,1)S(1)} async-done(((bf16[64,3,1792]{2,1,0:T(4,128)(2,1)}), bf16[64,3,1792]{2,1,0:T(4,128)(2,1)S(1)}, u32[]{:S(2)}, u32[]{:S(2)}) %all-to-all-start) | async-done | bytes 688160 | tf_op jit(solution)/shard_map/all_to_all | solution.py:43
  59.8 0.1 broadcast_in_dim.41
  59.9 13.1 %all_to_all.25 = bf16[2,64,3,1792]{3,1,2,0:T(8,128)(2,1)S(1)} all-to-all(bf16[2,64,3,1792]{3,1,2,0:T(8,128)(2,1)S(1)} %broadcast_in_dim.41), channel_id=1, replica_groups=mesh['groups'=2,'expert_0'=8,'expert_1'=8,'tensor'=2] {'tensor'}, dimensions={0} | all-to-all | bytes 2752512 | tf_op jit(solution)/shard_map/all_to_all | solution.py:23
  73.0 1.4 copy.56
  74.4 0.1 copy.74
  74.5 0.5 copy-done.1
  75.0 0.9 fusion.2
  75.9 6.2 %all-gather.7.cloned.1.call-done = f32[8,66,512]{2,1,0:T(8,128)} async-done(((f32[1,66,512]{2,1,0:T(8,128)}), f32[8,66,512]{2,1,0:T(8,128)}) %all-gather.7.cloned.1.call-update) | async-done | bytes 1081360 | tf_op jit(solution)/shard_map/all_gather | solution.py:71
  82.1 1.0 fusion.89
  83.2 1.5 fusion.19
  84.7 0.7 maximum_bitcast_fusion.1
  85.4 2.9 %fusion.7 = bf16[192,512]{1,0:T(8,128)(2,1)S(1)} fusion(bf16[192,3584]{1,0:T(8,128)(2,1)S(1)} %bitcast.319, bf16[1,3584,512]{2,1,0:T(8,128)(2,1)} %param.17, f32[192,512]{1,0:T(8,128)S(1)} %fusion.2), kind=kOutput, calls=%fused_computation.8 | convolution fusion | flops 705232896 | bytes 5636096 | tf_op jit(solution)/shard_map/dot_general | solution.py:143
  88.3 0.1 dot_general.26
  88.5 3.4 %convolution_bitcast_fusion = f32[2,64,3,1792]{3,1,0,2:T(8,128)S(1)} fusion(bf16[2,1792,512,1]{2,1,0,3:T(8,128)(2,1)} %bitcast.317, bf16[64,3,512,1]{2,1,0,3:T(4,128)(2,1)S(1)} %bitcast.323), kind=kOutput, calls=%fused_computation.6 | convolution fusion | flops 704643072 | bytes 6619136 | tf_op jit(solution)/shard_map/dot_general | solution.py:145
  91.8 0.2 copy.59
  92.1 10.2 %all_to_all.26 = f32[2,64,3,1792]{3,1,2,0:T(8,128)S(1)} all-to-all(f32[2,64,3,1792]{3,1,2,0:T(8,128)S(1)} %copy.59), channel_id=1, replica_groups=mesh['groups'=2,'expert_0'=8,'expert_1'=8,'tensor'=2] {'tensor'}, dimensions={0} | all-to-all | bytes 5505024 | tf_op jit(solution)/shard_map/all_to_all | solution.py:59
  102.2 1.2 reduce_sum.40
  103.5 2.6 %copy.61 = bf16[64,3,1792]{2,1,0:T(4,128)(2,1)} copy(bf16[64,3,1792]{2,0,1:T(8,128)(2,1)} %reduce_sum.40) | data formatting | bytes 1376256 | tf_op jit(solution)/shard_map/convert_element_type | solution.py:152
  106.1 10.6 %all-to-all-start.3 = ((bf16[64,3,1792]{2,1,0:T(4,128)(2,1)}), bf16[64,3,1792]{2,1,0:T(4,128)(2,1)S(1)}, u32[]{:S(2)}, u32[]{:S(2)}) async-start(bf16[64,3,1792]{2,1,0:T(4,128)(2,1)} %copy.61), calls=%async_computation.3 | async-start | bytes 1835008 | tf_op jit(solution)/shard_map/all_to_all | solution.py:153
  116.7 30.1 %all-to-all-done.3 = bf16[64,3,1792]{2,1,0:T(4,128)(2,1)S(1)} async-done(((bf16[64,3,1792]{2,1,0:T(4,128)(2,1)}), bf16[64,3,1792]{2,1,0:T(4,128)(2,1)S(1)}, u32[]{:S(2)}, u32[]{:S(2)}) %all-to-all-start.3) | async-done | bytes 688160 | tf_op jit(solution)/shard_map/all_to_all | solution.py:153
  146.8 0.6 reshape.989
  147.4 0.9 gather_fusion
  148.4 0.4 fusion.12
  148.8 5.4 %all_to_all.27 = bf16[2,16,1792]{2,1,0:T(8,128)(2,1)S(1)} all-to-all(bf16[2,16,1792]{2,1,0:T(8,128)(2,1)S(1)} %broadcast_in_dim.43), channel_id=1, replica_groups=mesh['groups'=2,'expert_0'=8,'expert_1'=8,'tensor'=2] {'tensor'}, dimensions={0} | all-to-all | bytes 229376 | tf_op jit(solution)/shard_map/all_to_all | solution.py:23
  154.2 0.7 copy.73
  154.9 1.0 fusion.87
  157.3 1.4 fusion.88
  158.7 0.8 divide_convert_fusion
  (51 shorter events, 2.3 us)
Async XLA Ops:
  7.2 1.0 copy-start
  7.2 74.9 %all-gather.7.cloned.1.call-start = ((), (), s32[]{:S(2)}) async-start(), calls=%async_computation.5 | async-start | bytes 1327104 | tf_op jit(solution)/shard_map/all_gather | solution.py:71
  18.8 40.9 %all-to-all-start = ((bf16[64,3,1792]{2,1,0:T(4,128)(2,1)}), bf16[64,3,1792]{2,1,0:T(4,128)(2,1)S(1)}, u32[]{:S(2)}, u32[]{:S(2)}) async-start(bf16[64,3,1792]{2,1,0:T(4,128)(2,1)} %reshape.988), calls=%async_computation | async-start | bytes 1835008 | tf_op jit(solution)/shard_map/all_to_all | solution.py:43
  40.6 114.3 %all-gather.9.cloned.1.call-start = ((), (), s32[]{:S(2)}) async-start(), calls=%async_computation.6 | async-start | bytes 1327104 | tf_op jit(solution)/shard_map/all_gather | solution.py:71
  73.0 2.1 %copy-start.1 = (bf16[1,3584,512]{2,1,0:T(8,128)(2,1)S(1)}, bf16[1,3584,512]{2,1,0:T(8,128)(2,1)}, u32[]{:S(2)}) copy-start(bf16[1,3584,512]{2,1,0:T(8,128)(2,1)} %param.16) | copy-start | bytes 11010052
  102.2 14.4 %copy-start.2 = (s32[16,8]{0,1:T(8,128)S(1)}, s32[16,8]{0,1:T(8,128)}, u32[]{:S(2)}) copy-start(s32[16,8]{0,1:T(8,128)} %param.15) | copy-start | bytes 1540
  106.1 40.8 %all-to-all-start.3 = ((bf16[64,3,1792]{2,1,0:T(4,128)(2,1)}), bf16[64,3,1792]{2,1,0:T(4,128)(2,1)S(1)}, u32[]{:S(2)}, u32[]{:S(2)}) async-start(bf16[64,3,1792]{2,1,0:T(4,128)(2,1)} %copy.61), calls=%async_computation.3 | async-start | bytes 1835008 | tf_op jit(solution)/shard_map/all_to_all | solution.py:153
Sparse Core Ops, SparseCore 0:
  12.3 69.7 all-gather.6
  85.5 49.3 all-gather.8
where the time goes:
time: 167 us; the launch traced here: 166 us
  waiting for transfers between devices  49.5 us (30%)
  starting transfers between devices  32.5 us (19%)
  blocking collectives  28.6 us (17%)
  local copies, waits for them, and re-layouts  23.9 us (14%)
  between operations  15 us (9%)
  matrix products  9.37 us (6%)
  other arithmetic  7.51 us (4%)
    all_to_all x1, waiting for transfers between devices, local(): lax.all_to_all(share, EXPERT, split_axis=0, concat_axis=0, tiled=True)  30.1 us
    all_to_all x1, starting transfers between devices, exchange_in_groups(): lax.all_to_all(group, axis, split_axis=split_dim, concat_axis=concat_dim,...  21.8 us
    all_to_all x2, blocking collectives, sent_to_all(): return lax.all_to_all(copies, axis, split_axis=0, concat_axis=0, tiled=True)  18.5 us
    all_to_all x1, waiting for transfers between devices, exchange_in_groups(): lax.all_to_all(group, axis, split_axis=split_dim, concat_axis=concat_dim,...  13.1 us
    all_to_all x1, starting transfers between devices, local(): lax.all_to_all(share, EXPERT, split_axis=0, concat_axis=0, tiled=True)  10.6 us
    all_to_all x1, blocking collectives, summed_on_arrival(): lax.all_to_all(parts, axis, split_axis=0, concat_axis=0, tiled=True)  10.2 us
    all_gather x2, waiting for transfers between devices, collected_together(): both, at, found = (lax.all_gather(jnp.concatenate(lines), axis), 0, {})  6.21 us
    dot_general x2, local copies, waits for them, and re-layouts, expert_rows(): jnp.dot(hidden, w_down[0], preferred_element_type=jnp.float32)  6.04 us
  transfers between devices with their start and end apart: 4, of which 3 were waited for; matrix products, arithmetic and copies ran while one was open for 17% of the time, Pallas kernels for 0%

commit v1 on v0

v1 whole, which is shorter than its diff:
```python
import functools

import jax
import jax.numpy as jnp
from jax import lax
from jax.experimental import pallas as pl
from jax.experimental.pallas import tpu as pltpu
from jax.sharding import Mesh
from jax.sharding import PartitionSpec as P

MESH = pl.DeviceIdType.MESH
EXPERT = ("expert_0", "expert_1")
GROUPS_EXPERT = ("groups", "expert_0", "expert_1")
AXES = ("groups", "expert_0", "expert_1", "tensor")

gate_denominator = 1024.0
softmax_scale = 192.0 ** (-0.5)
SLOTS = 3
F32 = jnp.float32
BF16 = jnp.bfloat16


def split_widths(width, parts):
    unit = 256 if width % 256 == 0 else 128
    units = width // unit
    sizes = [units // parts + (1 if k < units % parts else 0) for k in range(parts)]
    return [s * unit for s in sizes if s]


def dot(a, b):
    return jnp.dot(a, b, preferred_element_type=F32)


def kernel(
    n,
    cd,
    cr,
    batch_ref,
    ctx_ref,
    idst_ref,
    ids_ref,
    gate_ref,
    hid_ref,
    wg_hbm,
    wu_hbm,
    wd_hbm,
    ql_ref,
    qr_ref,
    kl_ref,
    kr_ref,
    moe_ref,
    attn_ref,
    wg,
    wu,
    wdo,
    wdx,
    idr,
    gx,
    pk,
    xo,
    xx,
    px,
    pr,
    vb,
    vr,
    ub,
    ur,
    as0,
    ar0,
    as1,
    ar1,
    as2,
    acc,
    wsem,
    s_id,
    s_g,
    s_x,
    s_d,
    s_p,
    s_v,
    s_u,
    s_a,
    s_o,
):
    log = n.bit_length() - 1
    tok = hid_ref.shape[0]
    topk = ids_ref.shape[1]
    half = hid_ref.shape[1] // 2
    rows = n * n * SLOTS
    blk = n * SLOTS
    g = lax.axis_index("groups")
    y = lax.axis_index("expert_0")
    x = lax.axis_index("expert_1")
    c = lax.axis_index("tensor")
    A = y + c * (x - y)
    B = x + c * (y - x)
    sa = n + c * (1 - n)
    sb = 1 + c * (n - 1)
    order = sorted(range(1, n), key=lambda k: (-min(k, n - k), k))

    def on_a(off):
        p = lax.rem(A + off, n)
        return (g, p + c * (y - p), x + c * (p - x), c)

    def on_b(off):
        p = lax.rem(B + off, n)
        return (g, y + c * (p - y), p + c * (x - p), c)

    partner = (g, y, x, 1 - c)
    sent = []

    def copy(src, dst, sems, device):
        made = pltpu.make_async_remote_copy(
            src_ref=src,
            dst_ref=dst,
            send_sem=sems.at[0],
            recv_sem=sems.at[1],
            device_id=device,
            device_id_type=MESH,
        )
        sent.append(made)
        return made

    barrier = pltpu.get_barrier_semaphore()
    for off in order:
        pl.semaphore_signal(barrier, inc=1, device_id=on_a(off), device_id_type=MESH)
        pl.semaphore_signal(barrier, inc=1, device_id=on_b(off), device_id_type=MESH)
    pl.semaphore_signal(barrier, inc=1, device_id=partner, device_id_type=MESH)

    own = pl.multiple_of(c * half, 128)
    oth = pl.multiple_of((1 - c) * half, 128)
    loads = [
        pltpu.make_async_copy(wg_hbm.at[pl.ds(own, half), :], wg.at[0], wsem.at[0]),
        pltpu.make_async_copy(wu_hbm.at[pl.ds(own, half), :], wu.at[0], wsem.at[1]),
        pltpu.make_async_copy(wg_hbm.at[pl.ds(oth, half), :], wg.at[1], wsem.at[2]),
        pltpu.make_async_copy(wu_hbm.at[pl.ds(oth, half), :], wu.at[1], wsem.at[3]),
        pltpu.make_async_copy(wd_hbm.at[:, pl.ds(oth, half)], wdx, wsem.at[4]),
        pltpu.make_async_copy(wd_hbm.at[:, pl.ds(own, half)], wdo, wsem.at[5]),
    ]
    for load in loads:
        load.start()

    nb, nh, lat = ql_ref.shape
    ctx = kl_ref.shape[1]
    per = nb * nh // n
    first = (y * n + x) * ctx
    for b in range(nb):
        scores = lax.dot_general(
            ql_ref[b], kl_ref[b], (((1,), (1,)), ((), ())), preferred_element_type=F32
        )
        scores = scores + dot(qr_ref[b], kr_ref[b])
        position = first + lax.broadcasted_iota(jnp.int32, scores.shape, 1)
        valid = position < ctx_ref[b]
        scores = jnp.where(valid, scores * softmax_scale, -1e30)
        peak = jnp.max(scores, axis=1, keepdims=True)
        probs = jnp.where(valid, jnp.exp(scores - peak), 0.0)
        total = jnp.sum(probs, axis=1, keepdims=True)
        weighted = dot(probs.astype(BF16), kl_ref[b])
        lane = lax.broadcasted_iota(jnp.int32, (nh, 128), 1)
        stats = jnp.where(lane < 64, peak, total)
        for k in range(nh // per):
            as0[b * (nh // per) + k, :, :lat] = weighted[k * per : (k + 1) * per]
            as0[b * (nh // per) + k, :, lat:] = stats[k * per : (k + 1) * per]

    def joined(parts):
        peaks = [p[:, lat : lat + 1] for p in parts]
        totals = [p[:, lat + 64 : lat + 65] for p in parts]
        top = functools.reduce(jnp.maximum, peaks)
        scales = [jnp.exp(p - top) for p in peaks]
        total = sum(t * s for t, s in zip(totals, scales))
        weighted = sum(p[:, :lat] * s for p, s in zip(parts, scales))
        return top, total, weighted

    for q, (at, w) in enumerate(cd):
        gx[q][0] = hid_ref[:, pl.ds(pl.multiple_of(own + at, 128), w)]

    pl.semaphore_wait(barrier, 2 * (n - 1) + 1)

    id_copies = [copy(idst_ref, idr.at[off], s_id.at[:, off], on_a(off)) for off in order]
    for made in id_copies:
        made.start()
    g_copies = []
    for q, (at, w) in enumerate(cd):
        source = hid_ref.at[:, pl.ds(pl.multiple_of(own + at, 128), w)]
        g_copies.append(
            [copy(source, gx[q].at[off], s_g.at[:, q, off], on_a(off)) for off in order]
        )
        for made in g_copies[-1]:
            made.start()
    a0 = []
    for off in order:
        block = lax.rem(A + off, n)
        a0.append(copy(as0.at[block], ar0.at[off], s_a.at[:, 0, off], on_a(off)))
        a0[-1].start()

    r_col = lax.broadcasted_iota(jnp.int32, (rows, 1), 0)

    def parts_of(r):
        q = lax.shift_right_logical(r * 171, 9)
        return lax.shift_right_logical(q, log), q & (n - 1), r - q * SLOTS

    first_of, second_of, slot_of = parts_of(r_col)
    for made in id_copies:
        made.wait_recv()
    lines = n * tok
    lane_t = lax.broadcasted_iota(jnp.int32, (topk, lines), 1)
    line_ids = idst_ref[...]
    for off in range(1, n):
        line_ids = jnp.where(lane_t // tok == off, idr[off], line_ids)
    lane_1 = lax.broadcasted_iota(jnp.int32, (1, lines), 1)
    back = lane_1 // tok
    owner = sa * ((A - back + n) & (n - 1)) + sb * B
    live = owner * tok + (lane_1 & (tok - 1)) < batch_ref[0]
    wanted = sa * A + sb * ((B + first_of) & (n - 1))
    match = line_ids[0:1, :] == wanted
    for k in range(1, topk):
        match = match | (line_ids[k : k + 1, :] == wanted)
    match = match & live & (back == second_of)
    match = match.astype(F32)
    t_row = lax.broadcasted_iota(jnp.int32, (lines, lines), 0)
    t_col = lax.broadcasted_iota(jnp.int32, (lines, lines), 1)
    before = jnp.where(t_row < t_col, 1.0, 0.0).astype(BF16)
    rank = dot(match.astype(BF16), before)
    pick = jnp.where(rank == slot_of.astype(F32), match, 0.0).astype(BF16)

    swap_to = ((second_of << log) + first_of) * SLOTS + slot_of
    swap = jnp.where(lax.broadcasted_iota(jnp.int32, (rows, rows), 1) == swap_to, 1.0, 0.0).astype(
        BF16
    )

    x_copies = []
    for q, (at, w) in enumerate(cd):
        for made in g_copies[q]:
            made.wait_recv()
        packed = dot(pick, gx[q][...].reshape(lines, w))
        xo[q][0] = packed[:blk].astype(BF16)
        for off in range(1, n):
            pk[q][off] = packed[off * blk : (off + 1) * blk].astype(BF16)
        x_copies.append(
            [copy(pk[q].at[off], xo[q].at[off], s_x.at[:, q, off], on_b(off)) for off in order]
        )
        for made in x_copies[-1]:
            made.start()

    for made in a0:
        made.wait_recv()
    top, total, weighted = joined([as0[A]] + [ar0[off] for off in range(1, n)])
    lane = lax.broadcasted_iota(jnp.int32, (per, 128), 1)
    as1[:, :lat] = weighted
    as1[:, lat:] = jnp.where(lane < 64, top, total)
    a1 = [copy(as1, ar1.at[off], s_a.at[:, 1, off], on_b(off)) for off in order]
    for made in a1:
        made.start()

    ff = wg.shape[2]
    for load in loads[:4]:
        load.wait()
    for q, (at, w) in enumerate(cd):
        d_copies = [copy(xo[q].at[0], xx[q].at[0], s_d.at[:, q, 0], partner)]
        d_copies[0].start()
        for k, off in enumerate(reversed(order)):
            x_copies[q][len(order) - 1 - k].wait_recv()
            d_copies.append(copy(xo[q].at[off], xx[q].at[off], s_d.at[:, q, off], partner))
            d_copies[-1].start()
        mine = xo[q][...].reshape(rows, w)
        gate = dot(mine, wg[0, at : at + w, :])
        upper = dot(mine, wu[0, at : at + w, :])
        if q:
            gate = gate + acc[:, :ff]
            upper = upper + acc[:, ff:]
        for made in d_copies:
            made.wait_recv()
        other = dot(swap, xx[q][...].reshape(rows, w)).astype(BF16)
        gate = gate + dot(other, wg[1, at : at + w, :])
        upper = upper + dot(other, wu[1, at : at + w, :])
        if q < len(cd) - 1:
            acc[:, :ff] = gate
            acc[:, ff:] = upper
    hidden = (gate / (1.0 + jnp.exp(-gate)) * upper).astype(BF16)
    turned = dot(swap, hidden).astype(BF16)

    loads[4].wait()
    loads[5].wait()
    p_copies = []
    for q, (at, w) in enumerate(cr):
        px[q][...] = dot(turned, wdx[:, at : at + w])
        p_copies.append(copy(px[q], pr[q], s_p.at[:, q], partner))
        p_copies[-1].start()
    v_copies = []
    for q, (at, w) in enumerate(cr):
        value = dot(hidden, wdo[:, at : at + w])
        p_copies[q].wait_recv()
        value = value + pr[q][...]
        vr[q][0] = value[:blk].astype(BF16)
        for off in range(1, n):
            vb[q][off] = value[off * blk : (off + 1) * blk].astype(BF16)
        v_copies.append(
            [copy(vb[q].at[off], vr[q].at[off], s_v.at[:, q, off], on_b(n - off)) for off in order]
        )
        for made in v_copies[-1]:
            made.start()

    for made in a1:
        made.wait_recv()
    top, total, weighted = joined([as1[...]] + [ar1[off] for off in range(1, n)])
    as2[A] = (weighted / total).astype(BF16)
    a2 = [copy(as2.at[A], as2.at[A], s_a.at[:, 2, off], on_a(off)) for off in order]
    for made in a2:
        made.start()

    r_lane = lax.broadcasted_iota(jnp.int32, (1, rows), 1)
    first_l, second_l, slot_l = parts_of(r_lane)
    named = sa * ((A + first_l) & (n - 1)) + sb * ((B + second_l) & (n - 1))
    ids = ids_ref[...]
    gates = gate_ref[...].astype(F32) / gate_denominator
    here = jnp.zeros((tok, rows), F32)
    weight = jnp.zeros((tok, rows), F32)
    for k in range(topk):
        same = ids[:, k : k + 1] == named
        here = jnp.where(same, 1.0, here)
        weight = jnp.where(same, gates[:, k : k + 1], weight)
    token = (sa * A + sb * B) * tok + lax.broadcasted_iota(jnp.int32, (tok, 1), 0)
    token_live = token < batch_ref[0]
    here = jnp.where(token_live, here, 0.0)
    r_tok = lax.broadcasted_iota(jnp.int32, (tok, tok), 0)
    c_tok = lax.broadcasted_iota(jnp.int32, (tok, tok), 1)
    earlier = jnp.where(c_tok < r_tok, 1.0, 0.0).astype(BF16)
    rank = dot(earlier, here.astype(BF16))
    weight = jnp.where((rank == slot_l.astype(F32)) & (here > 0.0), weight, 0.0)
    high = weight.astype(BF16)
    low = (weight - high.astype(F32)).astype(BF16)

    u_copies = []
    for q, (at, w) in enumerate(cr):
        for made in v_copies[q]:
            made.wait_recv()
        back_rows = dot(swap, vr[q][...].reshape(rows, w))
        ur[q][0] = back_rows[:blk].astype(BF16)
        for off in range(1, n):
            ub[q][off] = back_rows[off * blk : (off + 1) * blk].astype(BF16)
        u_copies.append(
            [copy(ub[q].at[off], ur[q].at[off], s_u.at[:, q, off], on_a(n - off)) for off in order]
        )
        for made in u_copies[-1]:
            made.start()

    for made in a2:
        made.wait_recv()
    attn_ref[...] = as2[...].reshape(nb, nh, lat)

    o_copies = []
    for q, (at, w) in enumerate(cr):
        for made in u_copies[q]:
            made.wait_recv()
        arrived = ur[q][...].reshape(rows, w)
        here_at = pl.ds(pl.multiple_of(own + at, 128), w)
        moe_ref[:, here_at] = (dot(high, arrived) + dot(low, arrived)).astype(BF16)
        o_copies.append(
            copy(moe_ref.at[:, here_at], moe_ref.at[:, here_at], s_o.at[:, q], partner)
        )
        o_copies[-1].start()
    for made in o_copies:
        made.wait_recv()
    for made in sent:
        made.wait_send()


def starts(widths):
    at, found = 0, []
    for w in widths:
        found.append((at, w))
        at += w
    return found


def local(
    hidden_in,
    batch_len,
    expert_ids,
    gate_num,
    w_gate,
    w_up,
    w_down,
    q_latent,
    q_rope,
    kv_latent,
    kv_rope,
    ctx_len,
):
    n = lax.axis_size("expert_0")
    tok, width = hidden_in.shape
    half = width // 2
    ff = w_gate.shape[2]
    nb, nh, lat = q_latent.shape
    per = nb * nh // n
    blk = n * SLOTS
    rows = n * blk
    cd = starts(split_widths(half, 2))
    cr = starts(split_widths(half, 2))
    ids_t = jnp.tile(expert_ids.T, (1, n))
    vmem = pl.BlockSpec(memory_space=pltpu.VMEM)
    smem = pl.BlockSpec(memory_space=pltpu.SMEM)
    hbm = pl.BlockSpec(memory_space=pl.ANY)
    V = pltpu.VMEM
    dma = pltpu.SemaphoreType.DMA
    qd, qr = len(cd), len(cr)
    scratch = [
        V((2, half, ff), BF16),
        V((2, half, ff), BF16),
        V((ff, half), BF16),
        V((ff, half), BF16),
        V((n, *ids_t.shape), jnp.int32),
        [V((n, tok, w), BF16) for _, w in cd],
        [V((n, blk, w), BF16) for _, w in cd],
        [V((n, blk, w), BF16) for _, w in cd],
        [V((n, blk, w), BF16) for _, w in cd],
        [V((rows, w), F32) for _, w in cr],
        [V((rows, w), F32) for _, w in cr],
        [V((n, blk, w), BF16) for _, w in cr],
        [V((n, blk, w), BF16) for _, w in cr],
        [V((n, blk, w), BF16) for _, w in cr],
        [V((n, blk, w), BF16) for _, w in cr],
        V((n, per, lat + 128), F32),
        V((n, per, lat + 128), F32),
        V((per, lat + 128), F32),
        V((n, per, lat + 128), F32),
        V((n, per, lat), BF16),
        V((rows, 2 * ff), F32),
        dma((6,)),
        dma((2, n)),
        dma((2, qd, n)),
        dma((2, qd, n)),
        dma((2, qd, n)),
        dma((2, qr)),
        dma((2, qr, n)),
        dma((2, qr, n)),
        dma((2, 3, n)),
        dma((2, qr)),
    ]
    return pl.pallas_call(
        functools.partial(kernel, n, cd, cr),
        out_shape=(
            jax.ShapeDtypeStruct((tok, width), BF16),
            jax.ShapeDtypeStruct((nb, nh, lat), BF16),
        ),
        in_specs=[smem, smem, vmem, vmem, vmem, vmem, hbm, hbm, hbm, vmem, vmem, vmem, vmem],
        out_specs=(vmem, vmem),
        scratch_shapes=scratch,
        compiler_params=pltpu.CompilerParams(
            collective_id=0, has_side_effects=True, vmem_limit_bytes=56 * 1024 * 1024
        ),
        name="layer_step",
    )(
        batch_len,
        ctx_len,
        ids_t,
        expert_ids,
        gate_num,
        hidden_in,
        w_gate[0],
        w_up[0],
        w_down[0],
        q_latent,
        q_rope,
        kv_latent,
        kv_rope,
    )


def solution(mesh):
    owners = mesh.shape["expert"]
    side = 1
    while side * side < owners:
        side *= 2
    finer = Mesh(
        mesh.devices.reshape(mesh.shape["groups"], side, owners // side, mesh.shape["tensor"]),
        AXES,
    )
    in_specs = (
        P(GROUPS_EXPERT, None),
        P("groups"),
        P(GROUPS_EXPERT, None),
        P(GROUPS_EXPERT, None),
        P(EXPERT, None, "tensor"),
        P(EXPERT, None, "tensor"),
        P(EXPERT, "tensor", None),
        P("groups", "tensor", None),
        P("groups", "tensor", None),
        P("groups", EXPERT, None),
        P("groups", None, EXPERT),
        P("groups"),
    )
    out_specs = (P(GROUPS_EXPERT, None), P("groups", "tensor", None))
    return jax.shard_map(local, mesh=finer, in_specs=in_specs, out_specs=out_specs, check_vma=False)
```

time: 167 us -> 81.2 us (0.49)
  Pallas kernels: 0 us -> 72.5 us
  waiting for transfers between devices: 49.5 us -> 0 us
  starting transfers between devices: 32.5 us -> 0 us
  blocking collectives: 28.6 us -> 0 us
  local copies, waits for them, and re-layouts: 23.9 us -> 7.08 us
  between operations: 15 us -> 1.29 us
  matrix products: 9.37 us -> 0 us
  other arithmetic: 7.51 us -> 0 us
    pallas_call x0 -> x1, Pallas kernels: none -> 72.5 us  [local(): pl.pallas_call(functools.partial(kernel, n, cd, cr), out_shape=(jax.Shape...]
    all_to_all x2 -> x0, waiting for transfers between devices: 43.2 us -> none  [the longest x1 30.1 us: local(): lax.all_to_all(share, EXPERT, split_axis=0, concat_axis=0, tiled=True)]
    all_to_all x2 -> x0, starting transfers between devices: 32.3 us -> none  [the longest x1 21.8 us: exchange_in_groups(): lax.all_to_all(group, axis, split_axis=split_dim, concat_axis=concat_dim,...]
    all_to_all x3 -> x0, blocking collectives: 28.6 us -> none  [the longest x2 18.5 us: sent_to_all(): return lax.all_to_all(copies, axis, split_axis=0, concat_axis=0, tiled=True)]
    dot_general x6 -> x0, matrix products: 9.37 us -> none  [the longest x1 3.38 us: expert_rows(): jnp.dot(hidden, w_down[0], preferred_element_type=jnp.float32)]
    all_gather x2 -> x0, waiting for transfers between devices: 6.21 us -> none  [collected_together(): both, at, found = (lax.all_gather(jnp.concatenate(lines), axis), 0, {})]
    dot_general x2 -> x0, local copies, waits for them, and re-layouts: 6.04 us -> none  [expert_rows(): jnp.dot(hidden, w_down[0], preferred_element_type=jnp.float32)]
    unnamed x11 -> x4, local copies, waits for them, and re-layouts: 2.26 us -> 5.73 us
  transfers between devices with their start and end apart: 4 -> 0, of which waited for: 3 -> 0; matrix products, arithmetic and copies ran while one was open for 17% -> 0% of each run, Pallas kernels for 0% -> 0%
where the time goes in v1:
time: 81.2 us; the launch traced here: 80.9 us
  Pallas kernels  72.5 us (89%)
  local copies, waits for them, and re-layouts  7.08 us (9%)
  between operations  1.29 us (2%)
    pallas_call x1, Pallas kernels, local(): pl.pallas_call(functools.partial(kernel, n, cd, cr), out_shape=(jax.Shape...  72.5 us
    unnamed x4, local copies, waits for them, and re-layouts  5.73 us

profile of v1, /device:TPU:513, one launch (start us, length us, event | category | flops | bytes accessed | tf_op | source)
XLA Modules:
  0.0 80.9 jit_solution(4992612640731430173)
XLA Ops:
  1.3 1.4 %copy.15.gate_ref = s32[16,8]{1,0:T(8,128)} copy(s32[16,8]{0,1:T(8,128)} %param.15) | data formatting | bytes 1024 | tf_op args[3]
  2.6 1.4 %copy.14.ids_ref = s32[16,8]{1,0:T(8,128)} copy(s32[16,8]{0,1:T(8,128)} %param.14) | data formatting | bytes 1024 | tf_op args[2]
  4.0 0.7 tile.4
  4.7 0.7 tile.10.idst_ref
  5.3 72.5 %layer_step.1 = (bf16[16,3584]{1,0:T(8,128)(2,1)}, bf16[2,32,512]{2,1,0:T(8,128)(2,1)}) custom-call(s32[1]{0:T(128)S(6)} %copy.18.batch_ref, s32[2]{0:T(128)} %ctx_ref.1, s32[8,128]{1,0:T(8,128)} %tile.10.idst_ref, s32[16,8]{1,0:T(8,128)} %copy.14.ids_ref, s32[16,8]{1,0:T(8,128)} %copy.15.gate_ref, bf16[16,3584]{1,0:T(8,128)(2,1)} %hid_ref.1, ...), custom_call_target="tpu_custom_call" | custom-call | tf_op jit(solution)/shard_map/layer_step/pallas_call | solution.py:440
  77.8 1.6 %copy.19 = bf16[16,3584]{1,0:T(8,128)(2,1)} copy(bf16[16,3584]{1,0:T(8,128)(2,1)} %get-tuple-element.4) | data formatting | bytes 229376
  79.4 1.5 %copy.20 = bf16[2,32,512]{2,1,0:T(8,128)(2,1)} copy(bf16[2,32,512]{2,1,0:T(8,128)(2,1)} %get-tuple-element.5) | data formatting | bytes 131072

commit v2 on v1

v2 whole, which is shorter than its diff:
```python
import functools

import jax
import jax.numpy as jnp
from jax import lax
from jax.experimental import pallas as pl
from jax.experimental.pallas import tpu as pltpu
from jax.sharding import Mesh
from jax.sharding import PartitionSpec as P

MESH = pl.DeviceIdType.MESH
EXPERT = ("expert_0", "expert_1")
GROUPS_EXPERT = ("groups", "expert_0", "expert_1")
AXES = ("groups", "expert_0", "expert_1", "tensor")

gate_denominator = 1024.0
softmax_scale = 192.0 ** (-0.5)
SLOTS = 3
KEEP = True
ND = 3
NR = 3
F32 = jnp.float32
BF16 = jnp.bfloat16


def split_widths(width, parts):
    unit = 256 if width % 256 == 0 else 128
    units = width // unit
    sizes = [units // parts + (1 if k < units % parts else 0) for k in range(parts)]
    return [s * unit for s in sizes if s]


def dot(a, b):
    return jnp.dot(a, b, preferred_element_type=F32)


def kernel(
    n,
    cd,
    cr,
    batch_ref,
    ctx_hbm,
    ids_hbm,
    gate_hbm,
    hid_hbm,
    wg_hbm,
    wu_hbm,
    wd_hbm,
    ql_hbm,
    qr_hbm,
    kl_hbm,
    kr_hbm,
    moe_ref,
    attn_ref,
    ctx_ref,
    ids_ref,
    gate_ref,
    ql_ref,
    qr_ref,
    kl_ref,
    kr_ref,
    wg,
    wu,
    wdo,
    wdr,
    ids0,
    idr,
    gx,
    pk,
    xo,
    xx,
    hs,
    hr,
    va,
    vb,
    vr,
    ub,
    ur,
    as0,
    ar0,
    as1,
    ar1,
    as2,
    acc,
    lsem,
    s_w,
    s_id,
    s_g,
    s_x,
    s_d,
    s_h,
    s_v,
    s_u,
    s_a,
    s_o,
):
    log = n.bit_length() - 1
    topk, tok = ids_ref.shape
    ff = wg.shape[2]
    half = hid_hbm.shape[1] // 2
    rows = n * n * SLOTS
    blk = n * SLOTS
    lines = n * tok
    g = lax.axis_index("groups")
    y = lax.axis_index("expert_0")
    x = lax.axis_index("expert_1")
    c = lax.axis_index("tensor")
    A = y + c * (x - y)
    B = x + c * (y - x)
    sa = n + c * (1 - n)
    sb = 1 + c * (n - 1)
    order = sorted(range(1, n), key=lambda k: (-min(k, n - k), k))
    own = pl.multiple_of(c * half, 128)
    oth = pl.multiple_of((1 - c) * half, 128)

    def on_a(off):
        p = lax.rem(A + off, n)
        return (g, p + c * (y - p), x + c * (p - x), c)

    def on_b(off):
        p = lax.rem(B + off, n)
        return (g, y + c * (p - y), p + c * (x - p), c)

    partner = (g, y, x, 1 - c)
    sent = []

    def copy(src, dst, sems, device):
        made = pltpu.make_async_remote_copy(
            src_ref=src,
            dst_ref=dst,
            send_sem=sems.at[0],
            recv_sem=sems.at[1],
            device_id=device,
            device_id_type=MESH,
        )
        sent.append(made)
        return made

    def arrive(name, copies):
        with jax.named_scope(name):
            for made in copies:
                made.wait_recv()

    barrier = pltpu.get_barrier_semaphore()
    for off in order:
        pl.semaphore_signal(barrier, inc=1, device_id=on_a(off), device_id_type=MESH)
        pl.semaphore_signal(barrier, inc=1, device_id=on_b(off), device_id_type=MESH)
    pl.semaphore_signal(barrier, inc=1, device_id=partner, device_id_type=MESH)

    started = []

    def load(src, dst):
        made = pltpu.make_async_copy(src, dst, lsem.at[len(started)])
        made.start()
        started.append(made)
        return made

    hid_loads = []
    for q, (at, w) in enumerate(cd):
        here_at = pl.ds(pl.multiple_of(own + at, 128), w)
        hid_loads.append(load(hid_hbm.at[:, here_at], gx[q].at[0]))
    id_load = load(ids_hbm, ids_ref)
    small_loads = [load(ctx_hbm, ctx_ref), load(gate_hbm, gate_ref)]
    kv_loads = [
        load(ql_hbm, ql_ref),
        load(kl_hbm, kl_ref),
        load(qr_hbm, qr_ref),
        load(kr_hbm, kr_ref),
    ]

    lane_of = lax.broadcasted_iota(jnp.int32, (tok, lines), 1) & (tok - 1)
    spread = jnp.where(lax.broadcasted_iota(jnp.int32, (tok, lines), 0) == lane_of, 1.0, 0.0)
    spread = spread.astype(BF16)
    id_load.wait()
    my_ids = dot(ids_ref[...].astype(F32).astype(BF16), spread)
    ids0[...] = my_ids
    for made in hid_loads:
        made.wait()
    with jax.named_scope("barrier"):
        pl.semaphore_wait(barrier, 2 * (n - 1) + 1)

    id_copies = [copy(ids0, idr.at[off], s_id.at[:, off], on_a(off)) for off in order]
    for made in id_copies:
        made.start()
    g_copies = []
    for q, (at, w) in enumerate(cd):
        g_copies.append(
            [copy(gx[q].at[0], gx[q].at[off], s_g.at[:, q, off], on_a(off)) for off in order]
        )
        for made in g_copies[-1]:
            made.start()
    w_loads = [
        load(wg_hbm.at[pl.ds(own, half), :], wg.at[0]),
        load(wu_hbm.at[pl.ds(own, half), :], wu.at[0]),
        load(wg_hbm.at[pl.ds(oth, half), :], wg.at[1]),
        load(wu_hbm.at[pl.ds(oth, half), :], wu.at[1]),
        load(wd_hbm.at[:, pl.ds(own, half)], wdo),
    ]

    for made in small_loads + kv_loads:
        made.wait()
    nb, nh, lat = ql_ref.shape
    ctx = kl_ref.shape[1]
    per = nb * nh // n
    first = (y * n + x) * ctx
    for b in range(nb):
        scores = lax.dot_general(
            ql_ref[b], kl_ref[b], (((1,), (1,)), ((), ())), preferred_element_type=F32
        )
        scores = scores + dot(qr_ref[b], kr_ref[b])
        position = first + lax.broadcasted_iota(jnp.int32, scores.shape, 1)
        valid = position < ctx_ref[b]
        scores = jnp.where(valid, scores * softmax_scale, -1e30)
        peak = jnp.max(scores, axis=1, keepdims=True)
        probs = jnp.where(valid, jnp.exp(scores - peak), 0.0)
        total = jnp.sum(probs, axis=1, keepdims=True)
        weighted = dot(probs.astype(BF16), kl_ref[b])
        lane = lax.broadcasted_iota(jnp.int32, (nh, 128), 1)
        stats = jnp.where(lane < 64, peak, total)
        for k in range(nh // per):
            as0[b * (nh // per) + k, :, :lat] = weighted[k * per : (k + 1) * per]
            as0[b * (nh // per) + k, :, lat:] = stats[k * per : (k + 1) * per]
    a0 = []
    for off in order:
        block = lax.rem(A + off, n)
        a0.append(copy(as0.at[block], ar0.at[off], s_a.at[:, 0, off], on_a(off)))
        a0[-1].start()

    def joined(parts):
        peaks = [p[:, lat : lat + 1] for p in parts]
        totals = [p[:, lat + 64 : lat + 65] for p in parts]
        top = functools.reduce(jnp.maximum, peaks)
        scales = [jnp.exp(p - top) for p in peaks]
        total = sum(t * s for t, s in zip(totals, scales))
        weighted = sum(p[:, :lat] * s for p, s in zip(parts, scales))
        return top, total, weighted

    r_col = lax.broadcasted_iota(jnp.int32, (rows, 1), 0)

    def parts_of(r):
        q = lax.shift_right_logical(r * 171, 9)
        return lax.shift_right_logical(q, log), q & (n - 1), r - q * SLOTS

    first_of, second_of, slot_of = parts_of(r_col)
    arrive("ids", id_copies)
    lane_t = lax.broadcasted_iota(jnp.int32, (topk, lines), 1)
    line_ids = my_ids
    for off in range(1, n):
        line_ids = jnp.where(lane_t // tok == off, idr[off], line_ids)
    lane_1 = lax.broadcasted_iota(jnp.int32, (1, lines), 1)
    back = lane_1 // tok
    owner = sa * ((A - back + n) & (n - 1)) + sb * B
    live = owner * tok + (lane_1 & (tok - 1)) < batch_ref[0]
    wanted = (sa * A + sb * ((B + first_of) & (n - 1))).astype(F32)
    match = line_ids[0:1, :] == wanted
    for k in range(1, topk):
        match = match | (line_ids[k : k + 1, :] == wanted)
    match = match & live & (back == second_of)
    match = match.astype(F32)
    t_row = lax.broadcasted_iota(jnp.int32, (lines, lines), 0)
    t_col = lax.broadcasted_iota(jnp.int32, (lines, lines), 1)
    before = jnp.where(t_row < t_col, 1.0, 0.0).astype(BF16)
    rank = dot(match.astype(BF16), before)
    pick = jnp.where(rank == slot_of.astype(F32), match, 0.0).astype(BF16)

    swap_to = ((second_of << log) + first_of) * SLOTS + slot_of
    swap = jnp.where(lax.broadcasted_iota(jnp.int32, (rows, rows), 1) == swap_to, 1.0, 0.0).astype(
        BF16
    )

    x_copies = []
    for q, (at, w) in enumerate(cd):
        arrive(f"g{q}", g_copies[q])
        packed = dot(pick, gx[q][...].reshape(lines, w))
        xo[q][0] = packed[:blk].astype(BF16)
        for off in range(1, n):
            pk[q][off] = packed[off * blk : (off + 1) * blk].astype(BF16)
        x_copies.append(
            [copy(pk[q].at[off], xo[q].at[off], s_x.at[:, q, off], on_b(off)) for off in order]
        )
        for made in x_copies[-1]:
            made.start()

    w_copy = copy(wd_hbm.at[:, pl.ds(oth, half)], wdr, s_w, partner)
    w_copy.start()

    for made in w_loads:
        made.wait()
    for q, (at, w) in enumerate(cd):
        d_copies = [copy(xo[q].at[0], xx[q].at[0], s_d.at[:, q, 0], partner)]
        d_copies[0].start()
        for k, off in enumerate(reversed(order)):
            arrive(f"x{q}_{k}", [x_copies[q][len(order) - 1 - k]])
            d_copies.append(copy(xo[q].at[off], xx[q].at[off], s_d.at[:, q, off], partner))
            d_copies[-1].start()
        mine = xo[q][...].reshape(rows, w)
        gate = dot(mine, wg[0, at : at + w, :])
        upper = dot(mine, wu[0, at : at + w, :])
        if q:
            gate = gate + acc[:, :ff]
            upper = upper + acc[:, ff:]
        arrive(f"d{q}", d_copies)
        other = dot(swap, xx[q][...].reshape(rows, w)).astype(BF16)
        gate = gate + dot(other, wg[1, at : at + w, :])
        upper = upper + dot(other, wu[1, at : at + w, :])
        if q < len(cd) - 1:
            acc[:, :ff] = gate
            acc[:, ff:] = upper
    hidden = (gate / (1.0 + jnp.exp(-gate)) * upper).astype(BF16)
    hs[...] = hidden
    h_copy = copy(hs, hr, s_h, partner)
    h_copy.start()
    for q, (at, w) in enumerate(cr):
        va[q][...] = dot(hidden, wdo[:, at : at + w])
    arrive("a0", a0)
    top, total, weighted = joined([as0[A]] + [ar0[off] for off in range(1, n)])
    lane = lax.broadcasted_iota(jnp.int32, (per, 128), 1)
    as1[:, :lat] = weighted
    as1[:, lat:] = jnp.where(lane < 64, top, total)
    a1 = [copy(as1, ar1.at[off], s_a.at[:, 1, off], on_b(off)) for off in order]
    for made in a1:
        made.start()

    arrive("wcopy", [w_copy])
    arrive("h", [h_copy])
    turned = dot(swap, hr[...]).astype(BF16)

    v_copies = []
    for q, (at, w) in enumerate(cr):
        value = va[q][...] + dot(turned, wdr[:, at : at + w])
        vr[q][0] = value[:blk].astype(BF16)
        for off in range(1, n):
            vb[q][off] = value[off * blk : (off + 1) * blk].astype(BF16)
        v_copies.append(
            [copy(vb[q].at[off], vr[q].at[off], s_v.at[:, q, off], on_b(n - off)) for off in order]
        )
        for made in v_copies[-1]:
            made.start()

    named = (sa * ((A + first_of) & (n - 1)) + sb * ((B + second_of) & (n - 1))).astype(F32)
    gates = gate_ref[...]
    coarse = lax.shift_right_logical(gates, 5)
    fine = gates - coarse * 32
    coarse = dot(coarse.astype(F32).astype(BF16), spread)
    fine = dot(fine.astype(F32).astype(BF16), spread)
    my_gates = (coarse * 32.0 + fine) / gate_denominator
    here = jnp.zeros((rows, lines), F32)
    weight = jnp.zeros((rows, lines), F32)
    for k in range(topk):
        same = my_ids[k : k + 1, :] == named
        here = jnp.where(same, 1.0, here)
        weight = jnp.where(same, my_gates[k : k + 1, :], weight)
    token = (sa * A + sb * B) * tok + lane_1
    here = jnp.where((token < batch_ref[0]) & (lane_1 < tok), here, 0.0)
    rank = dot(here.astype(BF16), before)
    weight = jnp.where((rank == slot_of.astype(F32)) & (here > 0.0), weight, 0.0)
    weight = weight.T[:tok]
    high = weight.astype(BF16)
    low = (weight - high.astype(F32)).astype(BF16)

    u_copies = []
    for q, (at, w) in enumerate(cr):
        arrive(f"v{q}", v_copies[q])
        back_rows = dot(swap, vr[q][...].reshape(rows, w))
        ur[q][0] = back_rows[:blk].astype(BF16)
        for off in range(1, n):
            ub[q][off] = back_rows[off * blk : (off + 1) * blk].astype(BF16)
        u_copies.append(
            [copy(ub[q].at[off], ur[q].at[off], s_u.at[:, q, off], on_a(n - off)) for off in order]
        )
        for made in u_copies[-1]:
            made.start()
        if q:
            continue
        arrive("a1", a1)
        top, total, weighted = joined([as1[...]] + [ar1[off] for off in range(1, n)])
        as2[A] = (weighted / total).astype(BF16)
        a2 = [copy(as2.at[A], as2.at[A], s_a.at[:, 2, off], on_a(off)) for off in order]
        for made in a2:
            made.start()

    arrive("a2", a2)
    attn_ref[...] = as2[...].reshape(nb, nh, lat)

    o_copies = []
    for q, (at, w) in enumerate(cr):
        arrive(f"u{q}", u_copies[q])
        arrived = ur[q][...].reshape(rows, w)
        here_at = pl.ds(pl.multiple_of(own + at, 128), w)
        moe_ref[:, here_at] = (dot(high, arrived) + dot(low, arrived)).astype(BF16)
        o_copies.append(
            copy(moe_ref.at[:, here_at], moe_ref.at[:, here_at], s_o.at[:, q], partner)
        )
        o_copies[-1].start()
    arrive("o", o_copies)
    with jax.named_scope("sends"):
        for made in sent:
            made.wait_send()


def starts(widths):
    at, found = 0, []
    for w in widths:
        found.append((at, w))
        at += w
    return found


def local(
    hidden_in,
    batch_len,
    expert_ids,
    gate_num,
    w_gate,
    w_up,
    w_down,
    q_latent,
    q_rope,
    kv_latent,
    kv_rope,
    ctx_len,
):
    n = lax.axis_size("expert_0")
    tok, width = hidden_in.shape
    half = width // 2
    ff = w_gate.shape[2]
    nb, nh, lat = q_latent.shape
    per = nb * nh // n
    blk = n * SLOTS
    rows = n * blk
    cd = starts(split_widths(half, ND))
    cr = starts(split_widths(half, NR))
    topk = expert_ids.shape[1]
    lines = n * tok
    ctx = kv_latent.shape[1]
    hbm = pl.BlockSpec(memory_space=pltpu.HBM)
    vmem = pl.BlockSpec(memory_space=pltpu.VMEM)
    V = pltpu.VMEM
    dma = pltpu.SemaphoreType.DMA
    qd, qr = len(cd), len(cr)
    i32 = jnp.int32
    scratch = [
        pltpu.SMEM(ctx_len.shape, i32),
        V((topk, tok), i32),
        V((topk, tok), i32),
        V(q_latent.shape, BF16),
        V(q_rope.shape, BF16),
        V(kv_latent.shape, BF16),
        V(kv_rope.shape, BF16),
        V((2, half, ff), BF16),
        V((2, half, ff), BF16),
        V((ff, half), BF16),
        V((ff, half), BF16),
        V((topk, lines), F32),
        V((n, topk, lines), F32),
        [V((n, tok, w), BF16) for _, w in cd],
        [V((n, blk, w), BF16) for _, w in cd],
        [V((n, blk, w), BF16) for _, w in cd],
        [V((n, blk, w), BF16) for _, w in cd],
        V((rows, ff), BF16),
        V((rows, ff), BF16),
        [V((rows, w), F32) for _, w in cr],
        [V((n, blk, w), BF16) for _, w in cr],
        [V((n, blk, w), BF16) for _, w in cr],
        [V((n, blk, w), BF16) for _, w in cr],
        [V((n, blk, w), BF16) for _, w in cr],
        V((n, per, lat + 128), F32),
        V((n, per, lat + 128), F32),
        V((per, lat + 128), F32),
        V((n, per, lat + 128), F32),
        V((n, per, lat), BF16),
        V((rows, 2 * ff), F32),
        dma((qd + 12,)),
        dma((2,)),
        dma((2, n)),
        dma((2, qd, n)),
        dma((2, qd, n)),
        dma((2, qd, n)),
        dma((2,)),
        dma((2, qr, n)),
        dma((2, qr, n)),
        dma((2, 3, n)),
        dma((2, qr)),
    ]
    outs = (
        jax.ShapeDtypeStruct((tok, width), BF16),
        jax.ShapeDtypeStruct((nb, nh, lat), BF16),
    )
    return pl.pallas_call(
        functools.partial(kernel, n, cd, cr),
        out_shape=tuple(pltpu.VMEM(o.shape, o.dtype) for o in outs) if KEEP else outs,
        in_specs=[pl.BlockSpec(memory_space=pltpu.SMEM)] + [hbm] * 11,
        out_specs=(vmem, vmem),
        scratch_shapes=scratch,
        compiler_params=pltpu.CompilerParams(
            collective_id=0, has_side_effects=True, vmem_limit_bytes=52 * 1024 * 1024
        ),
        name="layer_step",
    )(
        batch_len,
        *(
            pltpu.with_memory_space_constraint(value, pltpu.HBM)
            for value in (
                ctx_len,
                expert_ids.T,
                gate_num.T,
                hidden_in,
                w_gate[0],
                w_up[0],
                w_down[0],
                q_latent,
                q_rope,
                kv_latent,
                kv_rope,
            )
        )
    )


def solution(mesh):
    owners = mesh.shape["expert"]
    side = 1
    while side * side < owners:
        side *= 2
    finer = Mesh(
        mesh.devices.reshape(mesh.shape["groups"], side, owners // side, mesh.shape["tensor"]),
        AXES,
    )
    in_specs = (
        P(GROUPS_EXPERT, None),
        P("groups"),
        P(GROUPS_EXPERT, None),
        P(GROUPS_EXPERT, None),
        P(EXPERT, None, "tensor"),
        P(EXPERT, None, "tensor"),
        P(EXPERT, "tensor", None),
        P("groups", "tensor", None),
        P("groups", "tensor", None),
        P("groups", EXPERT, None),
        P("groups", None, EXPERT),
        P("groups"),
    )
    out_specs = (P(GROUPS_EXPERT, None), P("groups", "tensor", None))
    return jax.shard_map(local, mesh=finer, in_specs=in_specs, out_specs=out_specs, check_vma=False)
```

time: 81.2 us -> 72.2 us (0.89)
  local copies, waits for them, and re-layouts: 7.08 us -> 1.28 us
  Pallas kernels: 72.5 us -> 69.5 us
    unnamed x4 -> x2, local copies, waits for them, and re-layouts: 5.73 us -> 1.28 us
    pallas_call x1, Pallas kernels: 72.5 us -> 69.5 us  [local(): pl.pallas_call(functools.partial(kernel, n, cd, cr), out_shape=tuple((plt...]
    another operation x2 -> x0, local copies, waits for them, and re-layouts: 1.35 us -> none  [local(): ids_t = jnp.tile(expert_ids.T, (1, n))]
where the time goes in v2:
time: 72.2 us; the launch traced here: 72 us
  Pallas kernels  69.5 us (96%)
  between operations  1.29 us (2%)
  local copies, waits for them, and re-layouts  1.28 us (2%)
    pallas_call x1, Pallas kernels, local(): pl.pallas_call(functools.partial(kernel, n, cd, cr), out_shape=tuple((plt...  69.5 us

profile of v2, /device:TPU:513, one launch (start us, length us, event | category | flops | bytes accessed | tf_op | source)
XLA Modules:
  0.0 72.0 jit_solution(17343952226272116609)
XLA Ops:
  1.3 69.5 %layer_step.1 = (bf16[16,3584]{1,0:T(8,128)(2,1)S(1)}, bf16[2,32,512]{2,1,0:T(8,128)(2,1)S(1)}) custom-call(s32[1]{0:T(128)S(6)} %copy.18.batch_ref, s32[2]{0:T(128)} %ctx_hbm.1, s32[8,16]{1,0:T(8,128)} %bitcast.8, s32[8,16]{1,0:T(8,128)} %bitcast.9, bf16[16,3584]{1,0:T(8,128)(2,1)} %hid_hbm.1, bf16[3584,512]{1,0:T(8,128)(2,1)} %bitcast.5, ...), custom_call_target="tpu_custom_call" | custom-call | tf_op jit(solution)/shard_map/layer_step/pallas_call | solution.py:489
  70.8 0.6 copy.16
  71.4 0.6 copy.17

commit v3 on v2

--- a/solution.py
+++ b/solution.py
@@ -15,10 +15,11 @@
 
 gate_denominator = 1024.0
 softmax_scale = 192.0 ** (-0.5)
-SLOTS = 3
 KEEP = True
-ND = 3
-NR = 3
+GROUPS = ((0, 2), (2, 3))
+ND = 2
+NR = 1
+THROTTLE = False
 F32 = jnp.float32
 BF16 = jnp.bfloat16
 
@@ -98,8 +99,6 @@
     topk, tok = ids_ref.shape
     ff = wg.shape[2]
     half = hid_hbm.shape[1] // 2
-    rows = n * n * SLOTS
-    blk = n * SLOTS
     lines = n * tok
     g = lax.axis_index("groups")
     y = lax.axis_index("expert_0")
@@ -196,6 +195,8 @@
         load(wu_hbm.at[pl.ds(oth, half), :], wu.at[1]),
         load(wd_hbm.at[:, pl.ds(own, half)], wdo),
     ]
+    w_copy = copy(wd_hbm.at[:, pl.ds(oth, half)], wdr, s_w, partner)
+    w_copy.start()
 
     for made in small_loads + kv_loads:
         made.wait()
@@ -235,163 +236,202 @@
         weighted = sum(p[:, :lat] * s for p, s in zip(parts, scales))
         return top, total, weighted
 
-    r_col = lax.broadcasted_iota(jnp.int32, (rows, 1), 0)
-
-    def parts_of(r):
-        q = lax.shift_right_logical(r * 171, 9)
-        return lax.shift_right_logical(q, log), q & (n - 1), r - q * SLOTS
-
-    first_of, second_of, slot_of = parts_of(r_col)
+    t_row = lax.broadcasted_iota(jnp.int32, (lines, lines), 0)
+    t_col = lax.broadcasted_iota(jnp.int32, (lines, lines), 1)
+    before = jnp.where(t_row < t_col, 1.0, 0.0).astype(BF16)
+    lane_1 = lax.broadcasted_iota(jnp.int32, (1, lines), 1)
+    back = lane_1 // tok
+    owner = sa * ((A - back + n) & (n - 1)) + sb * B
+    live = owner * tok + (lane_1 & (tok - 1)) < batch_ref[0]
     arrive("ids", id_copies)
     lane_t = lax.broadcasted_iota(jnp.int32, (topk, lines), 1)
     line_ids = my_ids
     for off in range(1, n):
         line_ids = jnp.where(lane_t // tok == off, idr[off], line_ids)
-    lane_1 = lax.broadcasted_iota(jnp.int32, (1, lines), 1)
-    back = lane_1 // tok
-    owner = sa * ((A - back + n) & (n - 1)) + sb * B
-    live = owner * tok + (lane_1 & (tok - 1)) < batch_ref[0]
-    wanted = (sa * A + sb * ((B + first_of) & (n - 1))).astype(F32)
-    match = line_ids[0:1, :] == wanted
-    for k in range(1, topk):
-        match = match | (line_ids[k : k + 1, :] == wanted)
-    match = match & live & (back == second_of)
-    match = match.astype(F32)
-    t_row = lax.broadcasted_iota(jnp.int32, (lines, lines), 0)
-    t_col = lax.broadcasted_iota(jnp.int32, (lines, lines), 1)
-    before = jnp.where(t_row < t_col, 1.0, 0.0).astype(BF16)
-    rank = dot(match.astype(BF16), before)
-    pick = jnp.where(rank == slot_of.astype(F32), match, 0.0).astype(BF16)
-
-    swap_to = ((second_of << log) + first_of) * SLOTS + slot_of
-    swap = jnp.where(lax.broadcasted_iota(jnp.int32, (rows, rows), 1) == swap_to, 1.0, 0.0).astype(
-        BF16
-    )
-
-    x_copies = []
-    for q, (at, w) in enumerate(cd):
+
+    picks, swaps, numbers = [], [], []
+    for low_slot, high_slot in GROUPS:
+        m = high_slot - low_slot
+        rows = n * n * m
+        r = lax.broadcasted_iota(jnp.int32, (rows, 1), 0)
+        pair = lax.shift_right_logical(r, m.bit_length() - 1)
+        first_of = lax.shift_right_logical(pair, log)
+        second_of = pair & (n - 1)
+        inner = r & (m - 1)
+        slot_of = (low_slot + inner).astype(F32)
+        numbers.append((first_of, second_of, slot_of))
+        wanted = (sa * A + sb * ((B + first_of) & (n - 1))).astype(F32)
+        match = line_ids[0:1, :] == wanted
+        for k in range(1, topk):
+            match = match | (line_ids[k : k + 1, :] == wanted)
+        match = (match & live & (back == second_of)).astype(F32)
+        rank = dot(match.astype(BF16), before)
+        picks.append(jnp.where(rank == slot_of, match, 0.0).astype(BF16))
+        swap_to = ((second_of << log) + first_of) * m + inner
+        r_lane = lax.broadcasted_iota(jnp.int32, (rows, rows), 1)
+        swaps.append(jnp.where(r_lane == swap_to, 1.0, 0.0).astype(BF16))
+
+    def stored(value, blk, mine, others):
+        mine[0] = value[:blk].astype(BF16)
+        for off in range(1, n):
+            others[off] = value[off * blk : (off + 1) * blk].astype(BF16)
+
+    nq = len(cd)
+    x_copies = [[None] * nq for _ in GROUPS]
+
+    def send_picked(k, q):
+        blk = n * (GROUPS[k][1] - GROUPS[k][0])
+        stored(dot(picks[k], gx[q][...].reshape(lines, cd[q][1])), blk, xo[k][q], pk[k][q])
+        x_copies[k][q] = [
+            copy(pk[k][q].at[off], xo[k][q].at[off], s_x.at[:, k * nq + q, off], on_b(off))
+            for off in order
+        ]
+        if k == 0 or not THROTTLE:
+            for made in x_copies[k][q]:
+                made.start()
+
+    for q in range(nq):
         arrive(f"g{q}", g_copies[q])
-        packed = dot(pick, gx[q][...].reshape(lines, w))
-        xo[q][0] = packed[:blk].astype(BF16)
-        for off in range(1, n):
-            pk[q][off] = packed[off * blk : (off + 1) * blk].astype(BF16)
-        x_copies.append(
-            [copy(pk[q].at[off], xo[q].at[off], s_x.at[:, q, off], on_b(off)) for off in order]
-        )
-        for made in x_copies[-1]:
-            made.start()
-
-    w_copy = copy(wd_hbm.at[:, pl.ds(oth, half)], wdr, s_w, partner)
-    w_copy.start()
-
-    for made in w_loads:
-        made.wait()
-    for q, (at, w) in enumerate(cd):
-        d_copies = [copy(xo[q].at[0], xx[q].at[0], s_d.at[:, q, 0], partner)]
-        d_copies[0].start()
-        for k, off in enumerate(reversed(order)):
-            arrive(f"x{q}_{k}", [x_copies[q][len(order) - 1 - k]])
-            d_copies.append(copy(xo[q].at[off], xx[q].at[off], s_d.at[:, q, off], partner))
-            d_copies[-1].start()
-        mine = xo[q][...].reshape(rows, w)
-        gate = dot(mine, wg[0, at : at + w, :])
-        upper = dot(mine, wu[0, at : at + w, :])
-        if q:
-            gate = gate + acc[:, :ff]
-            upper = upper + acc[:, ff:]
-        arrive(f"d{q}", d_copies)
-        other = dot(swap, xx[q][...].reshape(rows, w)).astype(BF16)
-        gate = gate + dot(other, wg[1, at : at + w, :])
-        upper = upper + dot(other, wu[1, at : at + w, :])
-        if q < len(cd) - 1:
-            acc[:, :ff] = gate
-            acc[:, ff:] = upper
-    hidden = (gate / (1.0 + jnp.exp(-gate)) * upper).astype(BF16)
-    hs[...] = hidden
-    h_copy = copy(hs, hr, s_h, partner)
-    h_copy.start()
-    for q, (at, w) in enumerate(cr):
-        va[q][...] = dot(hidden, wdo[:, at : at + w])
-    arrive("a0", a0)
-    top, total, weighted = joined([as0[A]] + [ar0[off] for off in range(1, n)])
-    lane = lax.broadcasted_iota(jnp.int32, (per, 128), 1)
-    as1[:, :lat] = weighted
-    as1[:, lat:] = jnp.where(lane < 64, top, total)
-    a1 = [copy(as1, ar1.at[off], s_a.at[:, 1, off], on_b(off)) for off in order]
-    for made in a1:
-        made.start()
-
-    arrive("wcopy", [w_copy])
-    arrive("h", [h_copy])
-    turned = dot(swap, hr[...]).astype(BF16)
+        send_picked(0, q)
+    for k in range(1, len(GROUPS)):
+        for q in range(nq):
+            send_picked(k, q)
+    with jax.named_scope("wload"):
+        for made in w_loads:
+            made.wait()
 
     v_copies = []
-    for q, (at, w) in enumerate(cr):
-        value = va[q][...] + dot(turned, wdr[:, at : at + w])
-        vr[q][0] = value[:blk].astype(BF16)
-        for off in range(1, n):
-            vb[q][off] = value[off * blk : (off + 1) * blk].astype(BF16)
-        v_copies.append(
-            [copy(vb[q].at[off], vr[q].at[off], s_v.at[:, q, off], on_b(n - off)) for off in order]
-        )
-        for made in v_copies[-1]:
-            made.start()
-
-    named = (sa * ((A + first_of) & (n - 1)) + sb * ((B + second_of) & (n - 1))).astype(F32)
+    for k, (low_slot, high_slot) in enumerate(GROUPS):
+        blk = n * (high_slot - low_slot)
+        rows = n * blk
+        for q, (at, w) in enumerate(cd):
+            at_q = k * nq + q
+            d_copies = [copy(xo[k][q].at[0], xx[k][q].at[0], s_d.at[:, at_q, 0], partner)]
+            d_copies[0].start()
+            for p, off in reversed(list(enumerate(order))):
+                arrive(f"x{k}{q}_{off}", [x_copies[k][q][p]])
+                d_copies.append(
+                    copy(xo[k][q].at[off], xx[k][q].at[off], s_d.at[:, at_q, off], partner)
+                )
+                d_copies[-1].start()
+            if THROTTLE and k == 0 and q == nq - 1:
+                for later in x_copies[1:]:
+                    for made in sum(later, []):
+                        made.start()
+            mine = xo[k][q][...].reshape(rows, w)
+            gate = dot(mine, wg[0, at : at + w, :])
+            upper = dot(mine, wu[0, at : at + w, :])
+            if q:
+                gate = gate + acc[:rows, :ff]
+                upper = upper + acc[:rows, ff:]
+            arrive(f"d{k}{q}", d_copies)
+            other = dot(swaps[k], xx[k][q][...].reshape(rows, w)).astype(BF16)
+            gate = gate + dot(other, wg[1, at : at + w, :])
+            upper = upper + dot(other, wu[1, at : at + w, :])
+            if q < nq - 1:
+                acc[:rows, :ff] = gate
+                acc[:rows, ff:] = upper
+        hidden = (gate / (1.0 + jnp.exp(-gate)) * upper).astype(BF16)
+        hs[k][...] = hidden
+        h_copy = copy(hs[k], hr[k], s_h.at[:, k], partner)
+        h_copy.start()
+        for q, (at, w) in enumerate(cr):
+            va[q][:rows] = dot(hidden, wdo[:, at : at + w])
+        if k == 0:
+            arrive("a0", a0)
+            top, total, weighted = joined([as0[A]] + [ar0[off] for off in range(1, n)])
+            lane = lax.broadcasted_iota(jnp.int32, (per, 128), 1)
+            as1[:, :lat] = weighted
+            as1[:, lat:] = jnp.where(lane < 64, top, total)
+            a1 = [copy(as1, ar1.at[off], s_a.at[:, 1, off], on_b(off)) for off in order]
+            for made in a1:
+                made.start()
+        if k == len(GROUPS) - 1:
+            arrive("a1", a1)
+            top, total, weighted = joined([as1[...]] + [ar1[off] for off in range(1, n)])
+            as2[A] = (weighted / total).astype(BF16)
+            a2 = [copy(as2.at[A], as2.at[A], s_a.at[:, 2, off], on_a(off)) for off in order]
+            for made in a2:
+                made.start()
+        if k == 0:
+            arrive("wcopy", [w_copy])
+        arrive(f"h{k}", [h_copy])
+        turned = dot(swaps[k], hr[k][...]).astype(BF16)
+        v_copies.append([])
+        for q, (at, w) in enumerate(cr):
+            value = va[q][:rows] + dot(turned, wdr[:, at : at + w])
+            stored(value, blk, vr[k][q], vb[k][q])
+            made_now = [
+                copy(
+                    vb[k][q].at[off],
+                    vr[k][q].at[off],
+                    s_v.at[:, k * len(cr) + q, off],
+                    on_b(n - off),
+                )
+                for off in order
+            ]
+            for made in made_now:
+                made.start()
+            v_copies[k].append(made_now)
     gates = gate_ref[...]
     coarse = lax.shift_right_logical(gates, 5)
     fine = gates - coarse * 32
     coarse = dot(coarse.astype(F32).astype(BF16), spread)
     fine = dot(fine.astype(F32).astype(BF16), spread)
     my_gates = (coarse * 32.0 + fine) / gate_denominator
-    here = jnp.zeros((rows, lines), F32)
-    weight = jnp.zeros((rows, lines), F32)
-    for k in range(topk):
-        same = my_ids[k : k + 1, :] == named
-        here = jnp.where(same, 1.0, here)
-        weight = jnp.where(same, my_gates[k : k + 1, :], weight)
     token = (sa * A + sb * B) * tok + lane_1
-    here = jnp.where((token < batch_ref[0]) & (lane_1 < tok), here, 0.0)
-    rank = dot(here.astype(BF16), before)
-    weight = jnp.where((rank == slot_of.astype(F32)) & (here > 0.0), weight, 0.0)
-    weight = weight.T[:tok]
-    high = weight.astype(BF16)
-    low = (weight - high.astype(F32)).astype(BF16)
+    mine_live = (token < batch_ref[0]) & (lane_1 < tok)
+    weights = []
+    for first_of, second_of, slot_of in numbers:
+        named = sa * ((A + first_of) & (n - 1)) + sb * ((B + second_of) & (n - 1))
+        named = named.astype(F32)
+        here = jnp.zeros((named.shape[0], lines), F32)
+        weight = jnp.zeros((named.shape[0], lines), F32)
+        for k in range(topk):
+            same = my_ids[k : k + 1, :] == named
+            here = jnp.where(same, 1.0, here)
+            weight = jnp.where(same, my_gates[k : k + 1, :], weight)
+        here = jnp.where(mine_live, here, 0.0)
+        rank = dot(here.astype(BF16), before)
+        weight = jnp.where((rank == slot_of) & (here > 0.0), weight, 0.0)
+        weight = weight.T[:tok]
+        high = weight.astype(BF16)
+        weights.append((high, (weight - high.astype(F32)).astype(BF16)))
 
     u_copies = []
-    for q, (at, w) in enumerate(cr):
-        arrive(f"v{q}", v_copies[q])
-        back_rows = dot(swap, vr[q][...].reshape(rows, w))
-        ur[q][0] = back_rows[:blk].astype(BF16)
-        for off in range(1, n):
-            ub[q][off] = back_rows[off * blk : (off + 1) * blk].astype(BF16)
-        u_copies.append(
-            [copy(ub[q].at[off], ur[q].at[off], s_u.at[:, q, off], on_a(n - off)) for off in order]
-        )
-        for made in u_copies[-1]:
-            made.start()
-        if q:
-            continue
-        arrive("a1", a1)
-        top, total, weighted = joined([as1[...]] + [ar1[off] for off in range(1, n)])
-        as2[A] = (weighted / total).astype(BF16)
-        a2 = [copy(as2.at[A], as2.at[A], s_a.at[:, 2, off], on_a(off)) for off in order]
-        for made in a2:
-            made.start()
-
-    arrive("a2", a2)
-    attn_ref[...] = as2[...].reshape(nb, nh, lat)
-
+    for k, (low_slot, high_slot) in enumerate(GROUPS):
+        blk = n * (high_slot - low_slot)
+        u_copies.append([])
+        for q, (at, w) in enumerate(cr):
+            arrive(f"v{k}{q}", v_copies[k][q])
+            stored(dot(swaps[k], vr[k][q][...].reshape(n * blk, w)), blk, ur[k][q], ub[k][q])
+            made_now = [
+                copy(
+                    ub[k][q].at[off],
+                    ur[k][q].at[off],
+                    s_u.at[:, k * len(cr) + q, off],
+                    on_a(n - off),
+                )
+                for off in order
+            ]
+            for made in made_now:
+                made.start()
+            u_copies[k].append(made_now)
     o_copies = []
     for q, (at, w) in enumerate(cr):
-        arrive(f"u{q}", u_copies[q])
-        arrived = ur[q][...].reshape(rows, w)
+        summed = jnp.zeros((tok, w), F32)
+        for k, (high, low) in enumerate(weights):
+            arrive(f"u{k}{q}", u_copies[k][q])
+            arrived = ur[k][q][...].reshape(high.shape[1], w)
+            summed = summed + dot(high, arrived) + dot(low, arrived)
         here_at = pl.ds(pl.multiple_of(own + at, 128), w)
-        moe_ref[:, here_at] = (dot(high, arrived) + dot(low, arrived)).astype(BF16)
+        moe_ref[:, here_at] = summed.astype(BF16)
         o_copies.append(
             copy(moe_ref.at[:, here_at], moe_ref.at[:, here_at], s_o.at[:, q], partner)
         )
         o_copies[-1].start()
+    arrive("a2", a2)
+    attn_ref[...] = as2[...].reshape(nb, nh, lat)
     arrive("o", o_copies)
     with jax.named_scope("sends"):
         for made in sent:
@@ -426,8 +466,8 @@
     ff = w_gate.shape[2]
     nb, nh, lat = q_latent.shape
     per = nb * nh // n
-    blk = n * SLOTS
-    rows = n * blk
+    blks = [n * (high - low) for low, high in GROUPS]
+    most = n * max(blks)
     cd = starts(split_widths(half, ND))
     cr = starts(split_widths(half, NR))
     topk = expert_ids.shape[1]
@@ -439,6 +479,7 @@
     dma = pltpu.SemaphoreType.DMA
     qd, qr = len(cd), len(cr)
     i32 = jnp.int32
+    kk = len(GROUPS)
     scratch = [
         pltpu.SMEM(ctx_len.shape, i32),
         V((topk, tok), i32),
@@ -454,31 +495,31 @@
         V((topk, lines), F32),
         V((n, topk, lines), F32),
         [V((n, tok, w), BF16) for _, w in cd],
-        [V((n, blk, w), BF16) for _, w in cd],
-        [V((n, blk, w), BF16) for _, w in cd],
-        [V((n, blk, w), BF16) for _, w in cd],
-        V((rows, ff), BF16),
-        V((rows, ff), BF16),
-        [V((rows, w), F32) for _, w in cr],
-        [V((n, blk, w), BF16) for _, w in cr],
-        [V((n, blk, w), BF16) for _, w in cr],
-        [V((n, blk, w), BF16) for _, w in cr],
-        [V((n, blk, w), BF16) for _, w in cr],
+        [[V((n, blk, w), BF16) for _, w in cd] for blk in blks],
+        [[V((n, blk, w), BF16) for _, w in cd] for blk in blks],
+        [[V((n, blk, w), BF16) for _, w in cd] for blk in blks],
+        [V((n * blk, ff), BF16) for blk in blks],
+        [V((n * blk, ff), BF16) for blk in blks],
+        [V((most, w), F32) for _, w in cr],
+        [[V((n, blk, w), BF16) for _, w in cr] for blk in blks],
+        [[V((n, blk, w), BF16) for _, w in cr] for blk in blks],
+        [[V((n, blk, w), BF16) for _, w in cr] for blk in blks],
+        [[V((n, blk, w), BF16) for _, w in cr] for blk in blks],
         V((n, per, lat + 128), F32),
         V((n, per, lat + 128), F32),
         V((per, lat + 128), F32),
         V((n, per, lat + 128), F32),
         V((n, per, lat), BF16),
-        V((rows, 2 * ff), F32),
+        V((most, 2 * ff), F32),
         dma((qd + 12,)),
         dma((2,)),
         dma((2, n)),
         dma((2, qd, n)),
-        dma((2, qd, n)),
-        dma((2, qd, n)),
-        dma((2,)),
-        dma((2, qr, n)),
-        dma((2, qr, n)),
+        dma((2, kk * qd, n)),
+        dma((2, kk * qd, n)),
+        dma((2, kk)),
+        dma((2, kk * qr, n)),
+        dma((2, kk * qr, n)),
         dma((2, 3, n)),
         dma((2, qr)),
     ]

time: 72.2 us -> 70.5 us (0.976)
  Pallas kernels: 69.5 us -> 67.8 us
    pallas_call x1, Pallas kernels: 69.5 us -> 67.8 us  [local(): pl.pallas_call(functools.partial(kernel, n, cd, cr), out_shape=tuple((plt...]
where the time goes in v3:
time: 70.5 us; the launch traced here: 70.4 us
  Pallas kernels  67.8 us (96%)
  between operations  1.29 us (2%)
  local copies, waits for them, and re-layouts  1.28 us (2%)
    pallas_call x1, Pallas kernels, local(): pl.pallas_call(functools.partial(kernel, n, cd, cr), out_shape=tuple((plt...  67.8 us

profile of v3, /device:TPU:513, one launch (start us, length us, event | category | flops | bytes accessed | tf_op | source)
XLA Modules:
  0.0 70.4 jit_solution(6536049354274602779)
XLA Ops:
  1.3 67.8 %layer_step.1 = (bf16[16,3584]{1,0:T(8,128)(2,1)S(1)}, bf16[2,32,512]{2,1,0:T(8,128)(2,1)S(1)}) custom-call(s32[1]{0:T(128)S(6)} %copy.18.batch_ref, s32[2]{0:T(128)} %ctx_hbm.1, s32[8,16]{1,0:T(8,128)} %bitcast.8, s32[8,16]{1,0:T(8,128)} %bitcast.9, bf16[16,3584]{1,0:T(8,128)(2,1)} %hid_hbm.1, bf16[3584,512]{1,0:T(8,128)(2,1)} %bitcast.5, ...), custom_call_target="tpu_custom_call" | custom-call | tf_op jit(solution)/shard_map/layer_step/pallas_call | solution.py:530
  69.1 0.6 copy.16
  69.7 0.6 copy.17
